TPU v7x, 32 devices: a whole 2x2x4 slice. The times are simulated.
32 devices in a mesh: row: 4 (over y, x), col: 8 (over z, core).
Axes of the slice: x: 2, y: 2, z: 4, core: 2. Of those that a mesh axis runs over, the one named last changes fastest.
Arguments:
- view_one: bfloat16 [2048, 8192], P('row', 'col'), may hold values from -6 to 6
- view_two: bfloat16 [2048, 8192], P('row', 'col'), may hold values from -6 to 6
- pair_weights: bfloat16 [8192, 8192], P('row', 'col'), may hold values from 0.25 to 2.5
Outputs:
- first_grad: bfloat16 [2048, 8192], P('row', 'col')
- second_grad: bfloat16 [2048, 8192], P('row', 'col')
All inputs are finite; a program needn't handle non-finite values.
Results may differ from a plain program's by a relative error of at most 0.004.
Values may be sent and summed in bfloat16 or wider, within the bound.
A program may use at most 128 MiB of HBM per device.

v0:
```python
import jax
import jax.numpy as jnp
from jax import lax
from jax.sharding import PartitionSpec as P


def per_device(view_one, view_two, pair_weights):
    wide_two = lax.all_gather(view_two, "col", axis=1, tiled=True)
    samples = view_one.shape[0] * lax.axis_size("row")
    local_rows = pair_weights.shape[0]
    local_cols = pair_weights.shape[1]
    regrouped = lax.all_to_all(wide_two, "row", split_axis=1, concat_axis=0, tiled=True)
    summed = lax.dot_general(
        regrouped,
        lax.all_gather(view_one, "row", axis=0, tiled=True),
        (((0,), (0,)), ((), ())),
        preferred_element_type=jnp.float32,
    )
    correlation = summed / samples
    row_ids = lax.axis_index("row") * local_rows + lax.broadcasted_iota(
        jnp.int32, (local_rows, local_cols), 0
    )
    col_ids = lax.axis_index("col") * local_cols + lax.broadcasted_iota(
        jnp.int32, (local_rows, local_cols), 1
    )
    identity = jnp.where(row_ids == col_ids, 1.0, 0.0).astype(jnp.float32)
    weighted = (pair_weights.astype(jnp.float32) * (correlation - identity)).astype(jnp.bfloat16)
    grad_cols = lax.all_gather(weighted, "row", axis=0, tiled=True)
    first_grad = jnp.dot(wide_two, grad_cols, preferred_element_type=jnp.float32).astype(
        jnp.bfloat16
    )
    second_flipped = lax.psum_scatter(
        lax.dot_general(
            grad_cols, view_one, (((1,), (1,)), ((), ())), preferred_element_type=jnp.float32
        ),
        "col",
        scatter_dimension=0,
        tiled=True,
    )
    return (first_grad, second_flipped.T.astype(jnp.bfloat16))


def solution(mesh):
    placed = (P("row", "col"), P("row", "col"), P("row", "col"))
    return jax.shard_map(
        per_device,
        mesh=mesh,
        in_specs=placed,
        out_specs=(P("row", "col"), P("row", "col")),
        check_vma=False,
    )
```

profile of v0, /device:TPU:0, one launch (start us, length us, event | category | flops | bytes accessed | tf_op | source)
XLA Modules:
  0.0 604.9 jit_solution(17463055193101031785)
XLA Ops:
  8.0 0.0 all-gather.4.cloned.1.call-start
  8.0 2.3 copy.9
  10.3 0.0 all-gather.4.cloned.1.call-update
  10.3 85.4 %all-gather.4.cloned.1.call-done = bf16[512,8192]{0,1:T(8,128)(2,1)} async-done(((bf16[512,1024]{0,1:T(8,128)(2,1)}), bf16[512,8192]{0,1:T(8,128)(2,1)}) %all-gather.4.cloned.1.call-update) | async-done | bytes 8388624 | tf_op jit(solution)/shard_map/all_gather | solution.py:8
  95.8 5.7 all-to-all-start
  101.4 0.0 all-gather.6.cloned.1.call-start
  101.5 0.5 all-gather.6.cloned.1.call-update
  102.0 0.0 all-gather.8.cloned.1.call-start
  102.1 126.1 %all-to-all-done = bf16[512,4,2048]{0,2,1:T(8,128)(2,1)} async-done(((bf16[512,4,2048]{0,2,1:T(8,128)(2,1)}), bf16[512,4,2048]{0,2,1:T(8,128)(2,1)}, u32[]{:S(2)}, u32[]{:S(2)}) %all-to-all-start) | async-done | bytes 8388640 | tf_op jit(solution)/shard_map/all_to_all | solution.py:12
  228.2 11.4 %copy.10 = bf16[4,512,2048]{2,1,0:T(8,128)(2,1)} copy(bf16[4,512,2048]{1,2,0:T(8,128)(2,1)} %bitcast.1) | data formatting | bytes 16777216 | tf_op jit(solution)/shard_map/all_to_all | solution.py:12
  239.6 0.0 all-gather.6.cloned.1.call-done
  239.6 0.0 copy-start
  239.6 15.8 %multiply_convert_fusion = bf16[2048,1024]{1,0:T(8,128)(2,1)} fusion(bf16[2048,1024]{1,0:T(8,128)(2,1)} %param.5, bf16[2048,2048]{1,0:T(8,128)(2,1)} %bitcast.14, bf16[2048,1024]{1,0:T(8,128)(2,1)} %all-gather.6.cloned.1.call-done, s32[1024]{0:T(1024)S(1)} %iota_add_fusion.1, s32[2048]{0:T(1024)S(1)} %iota_add_fusion), kind=kOutput, calls=%fused_computation | convolution fusion | flops 8604614656 | bytes 20983808 | tf_op jit(solution)/shard_map/dot_general | solution.py:13
  255.4 0.0 all-gather.8.cloned.1.call-update
  255.4 0.2 reduce-scatter.2.cloned.1.call-start
  255.7 154.6 %all-gather.8.cloned.1.call-done = bf16[8192,1024]{1,0:T(8,128)(2,1)} async-done(((bf16[2048,1024]{1,0:T(8,128)(2,1)}), bf16[8192,1024]{1,0:T(8,128)(2,1)}) %all-gather.8.cloned.1.call-update) | async-done | bytes 16777232 | tf_op jit(solution)/shard_map/all_gather | solution.py:28
  410.3 0.0 copy-done
  410.3 15.8 %fusion.1 = f32[8192,512]{1,0:T(8,128)} fusion(bf16[8192,1024]{1,0:T(8,128)(2,1)} %all-gather.8.cloned.1.call-done, bf16[512,1024]{1,0:T(8,128)(2,1)S(1)} %copy-done), kind=kOutput, calls=%fused_computation.6 | convolution fusion | flops 8589934592 | bytes 34603008 | tf_op jit(solution)/shard_map/dot_general | solution.py:33
  426.0 0.0 reduce-scatter.2.cloned.1.call-update
  426.1 14.8 %fusion = bf16[512,1024]{0,1:T(8,128)(2,1)S(1)} fusion(bf16[8192,1024]{1,0:T(8,128)(2,1)} %all-gather.8.cloned.1.call-done, bf16[512,8192]{0,1:T(8,128)(2,1)} %all-gather.4.cloned.1.call-done), kind=kOutput, calls=%fused_computation.2 | convolution fusion | flops 8590458880 | bytes 26214400 | tf_op jit(solution)/shard_map/dot_general | solution.py:29
  440.9 1.3 copy.11
  442.2 152.2 %reduce-scatter.2.cloned.1.call-done = f32[1024,512]{1,0:T(8,128)} async-done(((f32[8192,512]{1,0:T(8,128)}), f32[1024,512]{1,0:T(8,128)}) %reduce-scatter.2.cloned.1.call-update) | async-done | bytes 2097168 | tf_op jit(solution)/shard_map/reduce_scatter | solution.py:32
  594.4 1.7 convert_bitcast_fusion
  596.1 1.3 copy.12
  (2 shorter events, 0.0 us)
Async XLA Ops:
  8.0 87.8 %all-gather.4.cloned.1.call-start = ((), (), s32[]{:S(2)}) async-start(), calls=%async_computation.2 | async-start | bytes 9437184 | tf_op jit(solution)/shard_map/all_gather | solution.py:8
  95.8 132.4 %all-to-all-start = ((bf16[512,4,2048]{0,2,1:T(8,128)(2,1)}), bf16[512,4,2048]{0,2,1:T(8,128)(2,1)}, u32[]{:S(2)}, u32[]{:S(2)}) async-start(bf16[512,4,2048]{0,2,1:T(8,128)(2,1)} %bitcast.13), calls=%async_computation | async-start | bytes 16777216 | tf_op jit(solution)/shard_map/all_to_all | solution.py:12
  101.4 138.2 %all-gather.6.cloned.1.call-start = ((), (), s32[]{:S(2)}) async-start(), calls=%async_computation.3 | async-start | bytes 5242880 | tf_op jit(solution)/shard_map/all_gather | solution.py:15
  102.0 308.3 %all-gather.8.cloned.1.call-start = ((), (), s32[]{:S(2)}) async-start(), calls=%async_computation.4 | async-start | bytes 20971520 | tf_op jit(solution)/shard_map/all_gather | solution.py:28
  239.6 170.7 %copy-start = (bf16[512,1024]{1,0:T(8,128)(2,1)S(1)}, bf16[512,1024]{1,0:T(8,128)(2,1)}, u32[]{:S(2)}) copy-start(bf16[512,1024]{1,0:T(8,128)(2,1)} %param.3) | copy-start | bytes 3145732
  255.4 339.0 %reduce-scatter.2.cloned.1.call-start = ((), (), s32[]{:S(2)}) async-start(), calls=%async_computation.5 | async-start | bytes 18874368 | tf_op jit(solution)/shard_map/reduce_scatter | solution.py:32
Sparse Core Ops, SparseCore 0:
  11.0 84.7 all-gather.3
  426.2 168.1 reduce-scatter.1
Sparse Core Ops, SparseCore 1:
  103.8 118.6 all-gather.5
  255.5 154.7 all-gather.7
where the time goes:
time: 605 us
  waiting for transfers between devices  519 us (86%)
  matrix products  46.4 us (8%)
  local copies, waits for them, and re-layouts  16.3 us (3%)
  between operations  15.5 us (3%)
    all_gather x1, waiting for transfers between devices, per_device(): grad_cols = lax.all_gather(weighted, 'row', axis=0, tiled=True)  155 us
    reduce_scatter x1, waiting for transfers between devices, per_device(): lax.psum_scatter(lax.dot_general(grad_cols, view_one, (((1,), (1,)), ((),...  152 us
    all_to_all x1, waiting for transfers between devices, per_device(): lax.all_to_all(wide_two, 'row', split_axis=1, concat_axis=0, tiled=True)  126 us
    all_gather x1, waiting for transfers between devices, per_device(): wide_two = lax.all_gather(view_two, 'col', axis=1, tiled=True)  85.4 us
    dot_general x1, matrix products, per_device(): lax.dot_general(regrouped, lax.all_gather(view_one, 'row', axis=0, tiled=...  15.8 us
    dot_general x1, matrix products, per_device(): lax.dot_general(grad_cols, view_one, (((1,), (1,)), ((), ())), preferred_...  15.8 us
    dot_general x1, matrix products, per_device(): jnp.dot(wide_two, grad_cols, preferred_element_type=jnp.float32)  14.8 us
  transfers between devices with their start and end apart: 5, of which 4 were waited for; matrix products, arithmetic and copies ran while one was open for 5% of the time, Pallas kernels for 0%

commit v1 on v0

--- a/solution.py
+++ b/solution.py
@@ -5,7 +5,7 @@
 
 
 def per_device(view_one, view_two, pair_weights):
-    wide_two = lax.all_gather(view_two, "col", axis=1, tiled=True)
+    wide_two = jnp.concatenate(lax.all_gather(view_two, "col"), axis=1)
     samples = view_one.shape[0] * lax.axis_size("row")
     local_rows = pair_weights.shape[0]
     local_cols = pair_weights.shape[1]

time: 605 us -> 616 us (1.018)
  local copies, waits for them, and re-layouts: 16.3 us -> 25.5 us
    reshape x0 -> x1, local copies, waits for them, and re-layouts: none -> 11.4 us  [per_device(): wide_two = jnp.concatenate(lax.all_gather(view_two, 'col'), axis=1)]
  transfers between devices with their start and end apart: 5 -> 5, of which waited for: 4 -> 4; matrix products, arithmetic and copies ran while one was open for 5% -> 4% of each run, Pallas kernels for 0% -> 0%
where the time goes in v1:
time: 616 us
  waiting for transfers between devices  521 us (85%)
  matrix products  46.4 us (8%)
  local copies, waits for them, and re-layouts  25.5 us (4%)
  between operations  15.5 us (3%)
    all_gather x1, waiting for transfers between devices, per_device(): grad_cols = lax.all_gather(weighted, 'row', axis=0, tiled=True)  155 us
    reduce_scatter x1, waiting for transfers between devices, per_device(): lax.psum_scatter(lax.dot_general(grad_cols, view_one, (((1,), (1,)), ((),...  152 us
    all_to_all x1, waiting for transfers between devices, per_device(): lax.all_to_all(wide_two, 'row', split_axis=1, concat_axis=0, tiled=True)  126 us
    all_gather x1, waiting for transfers between devices, per_device(): wide_two = jnp.concatenate(lax.all_gather(view_two, 'col'), axis=1)  86.5 us
    dot_general x1, matrix products, per_device(): lax.dot_general(regrouped, lax.all_gather(view_one, 'row', axis=0, tiled=...  15.8 us
    dot_general x1, matrix products, per_device(): lax.dot_general(grad_cols, view_one, (((1,), (1,)), ((), ())), preferred_...  15.8 us
    dot_general x1, matrix products, per_device(): jnp.dot(wide_two, grad_cols, preferred_element_type=jnp.float32)  14.8 us
  transfers between devices with their start and end apart: 5, of which 4 were waited for; matrix products, arithmetic and copies ran while one was open for 4% of the time, Pallas kernels for 0%

profile of v1, /device:TPU:0, one launch (start us, length us, event | category | flops | bytes accessed | tf_op | source)
XLA Modules:
  0.0 615.7 jit_solution(1238888336469507438)
XLA Ops:
  8.0 0.0 all-gather.9.cloned.1.call-start
  8.0 0.7 all-gather.9.cloned.1.call-update
  8.7 86.5 %all-gather.9.cloned.1.call-done = bf16[4096,1024]{1,0:T(8,128)(2,1)} async-done(((bf16[512,1024]{1,0:T(8,128)(2,1)}), bf16[4096,1024]{1,0:T(8,128)(2,1)}) %all-gather.9.cloned.1.call-update) | async-done | bytes 8388624 | tf_op jit(solution)/shard_map/all_gather | solution.py:8
  95.2 11.4 %copy.10 = bf16[512,8,1024]{0,2,1:T(8,128)(2,1)} copy(bf16[512,8,1024]{2,0,1:T(8,128)(2,1)} %bitcast.19) | data formatting | bytes 16777216 | tf_op jit(solution)/shard_map/reshape | solution.py:8
  106.6 5.7 all-to-all-start
  112.3 0.0 all-gather.5.cloned.1.call-start
  112.3 0.5 all-gather.5.cloned.1.call-update
  112.9 0.0 all-gather.7.cloned.1.call-start
  112.9 126.1 %all-to-all-done = bf16[512,4,2048]{0,2,1:T(8,128)(2,1)} async-done(((bf16[512,4,2048]{0,2,1:T(8,128)(2,1)}), bf16[512,4,2048]{0,2,1:T(8,128)(2,1)}, u32[]{:S(2)}, u32[]{:S(2)}) %all-to-all-start) | async-done | bytes 8388640 | tf_op jit(solution)/shard_map/all_to_all | solution.py:12
  239.0 11.4 %copy.11 = bf16[4,512,2048]{2,1,0:T(8,128)(2,1)} copy(bf16[4,512,2048]{1,2,0:T(8,128)(2,1)} %bitcast.3) | data formatting | bytes 16777216 | tf_op jit(solution)/shard_map/all_to_all | solution.py:12
  250.4 0.0 all-gather.5.cloned.1.call-done
  250.4 0.0 copy-start
  250.4 15.8 %multiply_convert_fusion = bf16[2048,1024]{1,0:T(8,128)(2,1)} fusion(bf16[2048,1024]{1,0:T(8,128)(2,1)} %param.5, bf16[2048,2048]{1,0:T(8,128)(2,1)} %bitcast.20, bf16[2048,1024]{1,0:T(8,128)(2,1)} %all-gather.5.cloned.1.call-done, s32[1024]{0:T(1024)S(1)} %iota_add_fusion.1, s32[2048]{0:T(1024)S(1)} %iota_add_fusion), kind=kOutput, calls=%fused_computation | convolution fusion | flops 8604614656 | bytes 20983808 | tf_op jit(solution)/shard_map/dot_general | solution.py:13
  266.3 0.0 all-gather.7.cloned.1.call-update
  266.3 0.2 reduce-scatter.2.cloned.1.call-start
  266.5 154.6 %all-gather.7.cloned.1.call-done = bf16[8192,1024]{1,0:T(8,128)(2,1)} async-done(((bf16[2048,1024]{1,0:T(8,128)(2,1)}), bf16[8192,1024]{1,0:T(8,128)(2,1)}) %all-gather.7.cloned.1.call-update) | async-done | bytes 16777232 | tf_op jit(solution)/shard_map/all_gather | solution.py:28
  421.1 0.0 copy-done
  421.1 15.8 %fusion.1 = f32[8192,512]{1,0:T(8,128)} fusion(bf16[8192,1024]{1,0:T(8,128)(2,1)} %all-gather.7.cloned.1.call-done, bf16[512,1024]{1,0:T(8,128)(2,1)S(1)} %copy-done), kind=kOutput, calls=%fused_computation.6 | convolution fusion | flops 8589934592 | bytes 34603008 | tf_op jit(solution)/shard_map/dot_general | solution.py:33
  436.9 0.0 reduce-scatter.2.cloned.1.call-update
  436.9 14.8 %fusion = bf16[512,1024]{0,1:T(8,128)(2,1)S(1)} fusion(bf16[8192,1024]{1,0:T(8,128)(2,1)} %all-gather.7.cloned.1.call-done, bf16[512,8192]{0,1:T(8,128)(2,1)} %bitcast.18), kind=kOutput, calls=%fused_computation.2 | convolution fusion | flops 8590458880 | bytes 26214400 | tf_op jit(solution)/shard_map/dot_general | solution.py:29
  451.7 1.3 copy.13
  453.1 152.2 %reduce-scatter.2.cloned.1.call-done = f32[1024,512]{1,0:T(8,128)} async-done(((f32[8192,512]{1,0:T(8,128)}), f32[1024,512]{1,0:T(8,128)}) %reduce-scatter.2.cloned.1.call-update) | async-done | bytes 2097168 | tf_op jit(solution)/shard_map/reduce_scatter | solution.py:32
  605.2 1.7 convert_bitcast_fusion
  607.0 1.3 copy.14
  (2 shorter events, 0.0 us)
Async XLA Ops:
  8.0 87.2 %all-gather.9.cloned.1.call-start = ((), (), s32[]{:S(2)}) async-start(), calls=%async_computation.5 | async-start | bytes 9437184 | tf_op jit(solution)/shard_map/all_gather | solution.py:8
  106.6 132.4 %all-to-all-start = ((bf16[512,4,2048]{0,2,1:T(8,128)(2,1)}), bf16[512,4,2048]{0,2,1:T(8,128)(2,1)}, u32[]{:S(2)}, u32[]{:S(2)}) async-start(bf16[512,4,2048]{0,2,1:T(8,128)(2,1)} %bitcast.17), calls=%async_computation | async-start | bytes 16777216 | tf_op jit(solution)/shard_map/all_to_all | solution.py:12
  112.3 138.2 %all-gather.5.cloned.1.call-start = ((), (), s32[]{:S(2)}) async-start(), calls=%async_computation.2 | async-start | bytes 5242880 | tf_op jit(solution)/shard_map/all_gather | solution.py:15
  112.9 308.3 %all-gather.7.cloned.1.call-start = ((), (), s32[]{:S(2)}) async-start(), calls=%async_computation.3 | async-start | bytes 20971520 | tf_op jit(solution)/shard_map/all_gather | solution.py:28
  250.4 170.7 %copy-start = (bf16[512,1024]{1,0:T(8,128)(2,1)S(1)}, bf16[512,1024]{1,0:T(8,128)(2,1)}, u32[]{:S(2)}) copy-start(bf16[512,1024]{1,0:T(8,128)(2,1)} %param.3) | copy-start | bytes 3145732
  266.3 339.0 %reduce-scatter.2.cloned.1.call-start = ((), (), s32[]{:S(2)}) async-start(), calls=%async_computation.4 | async-start | bytes 18874368 | tf_op jit(solution)/shard_map/reduce_scatter | solution.py:32
Sparse Core Ops, SparseCore 0:
  10.4 84.7 all-gather.8
  437.0 168.1 reduce-scatter.1
Sparse Core Ops, SparseCore 1:
  114.6 118.6 all-gather.4
  266.4 154.7 all-gather.6
